TPU v7x, 32 devices: a whole 2x2x4 slice. The times are simulated.
32 devices in a mesh: rep: 32 (over z, y, x, core).
Axes of the slice: x: 2, y: 2, z: 4, core: 2. Of those that a mesh axis runs over, the one named last changes fastest.
Arguments:
- inputs: bfloat16 [16384, 1024], P('rep'), may hold values from -6 to 6
- out_grads: bfloat16 [16384, 4096], P('rep'), may hold values from -0.29882812 to 0.29882812
- error_in: bfloat16 [32, 1024, 4096], P('rep'), may hold values from -6 to 6
- q_start: float32 [32, 4096], replicated, may hold values from -0.09375 to 0.09375
- master: float32 [1024, 4096], P(None, 'rep'), may hold values from -1.2 to 1.2
Outputs:
- error_out: bfloat16 [32, 1024, 4096], P('rep')
- q_out: float32 [32, 4096], replicated
- master_out: float32 [1024, 4096], P(None, 'rep')
All inputs are finite; a program needn't handle non-finite values.
Results may differ from a plain program's by a relative error of at most 0.001.
Values sent between devices are 32-bit elements; how exact they have to be, the bound alone decides.
No kernel may reach another device: no remote copies, remote signals or barrier semaphores. Data moves between devices by JAX's collectives and lax.ppermute only.
A program may use at most 128 MiB of HBM per device.

v0:
```python
import jax
import jax.numpy as jnp
from jax import lax
from jax.sharding import PartitionSpec as P

ITERS = 3


def orthonormal(rows):
    basis = jnp.zeros_like(rows)
    for k in range(rows.shape[0]):
        vector = rows[k]
        coef = jnp.dot(basis, vector, precision=lax.Precision.HIGHEST)
        vector = vector - jnp.dot(coef, basis, precision=lax.Precision.HIGHEST)
        basis = basis.at[k].set(vector / jnp.sqrt(jnp.sum(vector * vector) + 1.0))
    return basis


def outer_rows(left, right):
    return lax.dot_general(
        left,
        right,
        (((0,), (0,)), ((), ())),
        precision=lax.Precision.HIGHEST,
        preferred_element_type=jnp.float32,
    )


def shards(inputs, out_grads, error_in, q_start, master):
    count = lax.axis_size("rep")
    grad = lax.dot_general(
        inputs, out_grads, (((0,), (0,)), ((), ())), preferred_element_type=jnp.float32
    )
    merged = grad + error_in[0].astype(jnp.float32)
    factor = q_start
    basis = None
    local_q = None
    for step in range(ITERS):
        local_p = lax.dot_general(
            factor,
            merged,
            (((1,), (1,)), ((), ())),
            precision=lax.Precision.HIGHEST,
            preferred_element_type=jnp.float32,
        )
        total_p = lax.psum(local_p, "rep")
        basis = orthonormal(total_p)
        local_q = jnp.dot(
            basis, merged, precision=lax.Precision.HIGHEST, preferred_element_type=jnp.float32
        )
        if step + 1 < ITERS:
            factor = lax.psum(local_q, "rep") / count
    width = master.shape[1]
    factor = lax.psum(local_q, "rep") / count
    recon = outer_rows(basis, factor)
    own_cols = lax.dynamic_slice_in_dim(recon, lax.axis_index("rep") * width, width, 1)
    master_out = master - 0.5 * own_cols
    error_out = (merged - recon).astype(jnp.bfloat16)[None]
    return (error_out, factor, master_out)


def solution(mesh):
    return jax.shard_map(
        shards,
        mesh=mesh,
        in_specs=(P("rep", None), P("rep", None), P("rep", None, None), P(), P(None, "rep")),
        out_specs=(P("rep", None, None), P(), P(None, "rep")),
        check_vma=False,
    )
```

profile of v0, /device:TPU:0, one launch (start us, length us, event | category | flops | bytes accessed | tf_op | source)
XLA Modules:
  0.0 1167.3 jit_solution(7776026956208568537)
XLA Ops:
  7.2 1.2 copy-done
  8.4 8.8 convert_add_fusion
  17.2 5.7 copy-done.1
  22.9 16.0 %convolution_bitcast_fusion = f32[32,1024]{1,0:T(8,128)} fusion(f32[1024,4096]{1,0:T(8,128)S(1)} %convert_add_fusion, f32[32,4096]{1,0:T(8,128)S(1)} %copy-done.3), kind=kOutput, calls=%fused_computation.3 | convolution fusion | flops 1610612736 | bytes 17432576 | tf_op jit(solution)/shard_map/dot_general | solution.py:39
  39.1 127.2 %all-reduce.10.cloned.1.call-done = f32[32,1024]{1,0:T(8,128)} async-done(((f32[32,1024]{1,0:T(8,128)}), f32[32,1024]{1,0:T(8,128)}) %all-reduce.10.cloned.1.call-update) | async-done | bytes 131088 | tf_op jit(solution)/shard_map/psum | solution.py:46
  167.4 1.2 fusion.236
  172.4 0.9 convolution_bitcast_fusion.94
  175.0 0.9 convolution_bitcast_fusion.93
  180.2 0.9 convolution_bitcast_fusion.91
  185.4 0.9 convolution_bitcast_fusion.89
  190.5 0.9 convolution_bitcast_fusion.87
  195.7 0.9 convolution_bitcast_fusion.85
  198.3 0.9 convolution_bitcast_fusion.84
  200.9 0.9 convolution_bitcast_fusion.83
  202.1 1.3 fusion.235
  204.8 0.9 convolution_bitcast_fusion.82
  212.6 0.9 convolution_bitcast_fusion.79
  217.8 0.9 convolution_bitcast_fusion.77
  220.3 0.9 convolution_bitcast_fusion.76
  222.9 0.9 convolution_bitcast_fusion.75
  228.1 0.9 convolution_bitcast_fusion.73
  233.3 0.9 convolution_bitcast_fusion.71
  235.9 0.9 convolution_bitcast_fusion.70
  238.5 0.9 convolution_bitcast_fusion.69
  241.0 0.9 convolution_bitcast_fusion.68
  246.2 0.9 convolution_bitcast_fusion.66
  248.8 0.9 convolution_bitcast_fusion.65
  251.6 13.9 %fusion.267 = f32[32,4096]{1,0:T(8,128)} fusion(f32[32,1024]{1,0:T(8,128)S(1)} %scatter.371, f32[1024,4096]{1,0:T(8,128)} %copy-done.1), kind=kOutput, calls=%fused_computation.560 | convolution fusion | flops 1610612736 | bytes 17432576 | tf_op jit(solution)/shard_map/dot_general | solution.py:48
  265.6 128.2 %all-reduce.12.cloned.1.call-done = f32[32,4096]{1,0:T(8,128)} async-done(((f32[32,4096]{1,0:T(8,128)}), f32[32,4096]{1,0:T(8,128)}) %all-reduce.12.cloned.1.call-update) | async-done | bytes 524304 | tf_op jit(solution)/shard_map/psum | solution.py:52
  393.8 19.3 %fusion.3 = f32[32,1024]{1,0:T(8,128)} fusion(f32[1024,4096]{1,0:T(8,128)} %copy-done.1, f32[32,4096]{1,0:T(8,128)} %all-reduce.12.cloned.1.call-done), kind=kOutput, calls=%fused_computation.103 | convolution fusion | flops 1610743808 | bytes 17432576 | tf_op jit(solution)/shard_map/dot_general | solution.py:39
  413.2 123.6 %all-reduce.14.cloned.1.call-done = f32[32,1024]{1,0:T(8,128)} async-done(((f32[32,1024]{1,0:T(8,128)}), f32[32,1024]{1,0:T(8,128)}) %all-reduce.14.cloned.1.call-update) | async-done | bytes 131088 | tf_op jit(solution)/shard_map/psum | solution.py:46
  537.9 1.2 fusion.234
  542.9 0.9 convolution_bitcast_fusion.62
  545.5 0.9 convolution_bitcast_fusion.61
  550.7 0.9 convolution_bitcast_fusion.59
  553.3 0.9 convolution_bitcast_fusion.58
  573.0 1.3 fusion.233
  622.4 13.9 %fusion.298 = f32[32,4096]{1,0:T(8,128)} fusion(f32[32,1024]{1,0:T(8,128)S(1)} %scatter.425, f32[1024,4096]{1,0:T(8,128)} %copy-done.1), kind=kOutput, calls=%fused_computation.591 | convolution fusion | flops 1610612736 | bytes 17432576 | tf_op jit(solution)/shard_map/dot_general | solution.py:48
  636.5 128.1 %all-reduce.16.cloned.1.call-done = f32[32,4096]{1,0:T(8,128)} async-done(((f32[32,4096]{1,0:T(8,128)}), f32[32,4096]{1,0:T(8,128)}) %all-reduce.16.cloned.1.call-update) | async-done | bytes 524304 | tf_op jit(solution)/shard_map/psum | solution.py:52
  764.6 19.3 %fusion.1 = f32[32,1024]{1,0:T(8,128)} fusion(f32[1024,4096]{1,0:T(8,128)} %copy-done.1, f32[32,4096]{1,0:T(8,128)} %all-reduce.16.cloned.1.call-done), kind=kOutput, calls=%fused_computation.101 | convolution fusion | flops 1610743808 | bytes 17432576 | tf_op jit(solution)/shard_map/dot_general | solution.py:39
  784.0 123.6 %all-reduce.18.cloned.1.call-done = f32[32,1024]{1,0:T(8,128)} async-done(((f32[32,1024]{1,0:T(8,128)}), f32[32,1024]{1,0:T(8,128)}) %all-reduce.18.cloned.1.call-update) | async-done | bytes 131088 | tf_op jit(solution)/shard_map/psum | solution.py:46
  908.6 1.2 fusion.232
  943.3 1.3 fusion.231
  992.7 14.1 %fusion.329 = f32[32,4096]{1,0:T(8,128)} fusion(f32[32,1024]{1,0:T(8,128)S(1)} %scatter.479, f32[1024,4096]{1,0:T(8,128)} %copy-done.1), kind=kOutput, calls=%fused_computation.622 | convolution fusion | flops 1610612736 | bytes 17432576 | tf_op jit(solution)/shard_map/dot_general | solution.py:48
  1006.8 128.3 %all-reduce.20.cloned.1.call-done = f32[32,4096]{1,0:T(8,128)} async-done(((f32[32,4096]{1,0:T(8,128)}), f32[32,4096]{1,0:T(8,128)}) %all-reduce.20.cloned.1.call-update) | async-done | bytes 524304 | tf_op jit(solution)/shard_map/psum | solution.py:54
  1135.0 1.1 broadcast_multiply_fusion
  1136.1 13.6 %fusion.330 = f32[1024,4096]{1,0:T(8,128)S(1)} fusion(f32[32,1024]{1,0:T(8,128)S(1)} %scatter.479, f32[32,4096]{1,0:T(8,128)S(1)} %broadcast_multiply_fusion), kind=kOutput, calls=%fused_computation.623 | convolution fusion | flops 1610612736 | bytes 17432576 | tf_op jit(solution)/shard_map/dot_general | solution.py:20
  1149.7 9.6 fusion
  (477 shorter events, 158.8 us)
Async XLA Ops:
  7.2 1.2 copy-start
  7.2 15.7 %copy-start.3 = (f32[32,4096]{1,0:T(8,128)S(1)}, f32[32,4096]{1,0:T(8,128)}, u32[]{:S(2)}) copy-start(f32[32,4096]{1,0:T(8,128)} %param.200) | copy-start | bytes 1572868
  7.2 159.1 %all-reduce.10.cloned.1.call-start = ((), (), s32[]{:S(2)}) async-start(), calls=%async_computation | async-start | bytes 262144 | tf_op jit(solution)/shard_map/psum | solution.py:46
  17.2 5.7 copy-start.1
  38.9 354.9 %all-reduce.12.cloned.1.call-start = ((), (), s32[]{:S(2)}) async-start(), calls=%async_computation.1 | async-start | bytes 1048576 | tf_op jit(solution)/shard_map/psum | solution.py:52
  265.5 271.2 %all-reduce.14.cloned.1.call-start = ((), (), s32[]{:S(2)}) async-start(), calls=%async_computation.2 | async-start | bytes 262144 | tf_op jit(solution)/shard_map/psum | solution.py:46
  413.1 351.5 %all-reduce.16.cloned.1.call-start = ((), (), s32[]{:S(2)}) async-start(), calls=%async_computation.3 | async-start | bytes 1048576 | tf_op jit(solution)/shard_map/psum | solution.py:52
  636.3 271.2 %all-reduce.18.cloned.1.call-start = ((), (), s32[]{:S(2)}) async-start(), calls=%async_computation.4 | async-start | bytes 262144 | tf_op jit(solution)/shard_map/psum | solution.py:46
  783.9 351.1 %all-reduce.20.cloned.1.call-start = ((), (), s32[]{:S(2)}) async-start(), calls=%async_computation.5 | async-start | bytes 1048576 | tf_op jit(solution)/shard_map/psum | solution.py:54
  1136.1 23.2 %copy-start.2 = (f32[32,4096]{1,0:T(8,128)}, f32[32,4096]{1,0:T(8,128)S(1)}, u32[]{:S(2)}) copy-start(f32[32,4096]{1,0:T(8,128)S(1)} %broadcast_multiply_fusion) | copy-start | bytes 1572868
  1149.7 9.6 copy-start.4
Sparse Core Ops, SparseCore 0:
  39.0 127.2 all-reduce.9
  265.7 128.1 all-reduce.11
  413.3 123.4 all-reduce.13
  636.4 128.1 all-reduce.15
  784.0 123.4 all-reduce.17
  1006.9 128.0 all-reduce.19
where the time goes:
time: 1180 us; the launch traced here: 1170 us
  waiting for transfers between devices  759 us (64%)
  matrix products  229 us (19%)
  between operations  83.2 us (7%)
  other arithmetic  69.8 us (6%)
  local copies, waits for them, and re-layouts  25.2 us (2%)
    psum x3, waiting for transfers between devices, shards(): factor = lax.psum(local_q, 'rep') / count  385 us
    psum x3, waiting for transfers between devices, shards(): total_p = lax.psum(local_p, 'rep')  374 us
    dot_general x96, matrix products, orthonormal(): coef = jnp.dot(basis, vector, precision=lax.Precision.HIGHEST)  89.7 us
    reduce_sum x96, other arithmetic, orthonormal(): basis = basis.at[k].set(vector / jnp.sqrt(jnp.sum(vector * vector) + 1.0))  57.8 us
    dot_general x3, matrix products, shards(): lax.dot_general(factor, merged, (((1,), (1,)), ((), ())), precision=lax.P...  54.5 us
    dot_general x3, matrix products, shards(): jnp.dot(basis, merged, precision=lax.Precision.HIGHEST, preferred_element...  41.9 us
  transfers between devices with their start and end apart: 6, of which 6 were waited for; matrix products, arithmetic and copies ran while one was open for 0% of the time, Pallas kernels for 0%

commit v1 on v0

--- a/solution.py
+++ b/solution.py
@@ -43,7 +43,10 @@
             precision=lax.Precision.HIGHEST,
             preferred_element_type=jnp.float32,
         )
-        total_p = lax.psum(local_p, "rep")
+        n_dev, total_p = (lax.axis_size("rep"), local_p)
+        for hop in [1 << k_2 for k_2 in range(n_dev.bit_length() - 1)]:
+            pairs = [(i, i ^ hop) for i in range(n_dev)]
+            total_p = total_p + lax.ppermute(total_p, "rep", pairs)
         basis = orthonormal(total_p)
         local_q = jnp.dot(
             basis, merged, precision=lax.Precision.HIGHEST, preferred_element_type=jnp.float32

time: 1180 us -> 866 us (0.73)
  waiting for transfers between devices: 759 us -> 439 us
  starting transfers between devices: 0.59 us -> 23.4 us
    psum x3 -> x0, waiting for transfers between devices: 374 us -> none  [shards(): total_p = lax.psum(local_p, 'rep')]
    ppermute x0 -> x15, waiting for transfers between devices: none -> 51.9 us  [shards(): total_p = total_p + lax.ppermute(total_p, 'rep', pairs)]
    ppermute x0 -> x15, starting transfers between devices: none -> 23.1 us  [shards(): total_p = total_p + lax.ppermute(total_p, 'rep', pairs)]
  transfers between devices with their start and end apart: 6 -> 18, of which waited for: 6 -> 18; matrix products, arithmetic and copies ran while one was open for 0% -> 0% of each run, Pallas kernels for 0% -> 0%
where the time goes in v1:
time: 866 us; the launch traced here: 856 us
  waiting for transfers between devices  439 us (51%)
  matrix products  223 us (26%)
  between operations  83 us (10%)
  other arithmetic  70.1 us (8%)
  starting transfers between devices  23.4 us (3%)
  local copies, waits for them, and re-layouts  18 us (2%)
    psum x3, waiting for transfers between devices, shards(): factor = lax.psum(local_q, 'rep') / count  387 us
    dot_general x96, matrix products, orthonormal(): coef = jnp.dot(basis, vector, precision=lax.Precision.HIGHEST)  85.3 us
    reduce_sum x96, other arithmetic, orthonormal(): basis = basis.at[k].set(vector / jnp.sqrt(jnp.sum(vector * vector) + 1.0))  57.8 us
    dot_general x3, matrix products, shards(): lax.dot_general(factor, merged, (((1,), (1,)), ((), ())), precision=lax.P...  52.7 us
    ppermute x15, waiting for transfers between devices, shards(): total_p = total_p + lax.ppermute(total_p, 'rep', pairs)  51.9 us
    dot_general x3, matrix products, shards(): jnp.dot(basis, merged, precision=lax.Precision.HIGHEST, preferred_element...  41.9 us
    ppermute x15, starting transfers between devices, shards(): total_p = total_p + lax.ppermute(total_p, 'rep', pairs)  23.1 us
    dot_general x96, matrix products, orthonormal(): vector = vector - jnp.dot(coef, basis, precision=lax.Precision.HIGHEST)  20.9 us
  transfers between devices with their start and end apart: 18, of which 18 were waited for; matrix products, arithmetic and copies ran while one was open for 0% of the time, Pallas kernels for 0%

profile of v1, /device:TPU:0, one launch (start us, length us, event | category | flops | bytes accessed | tf_op | source)
XLA Modules:
  0.0 856.2 jit_solution(14471267732066899633)
XLA Ops:
  7.2 1.2 copy-done
  8.4 8.8 %convert_add_fusion = f32[1024,4096]{1,0:T(8,128)S(1)} fusion(bf16[1,1024,4096]{2,1,0:T(8,128)(2,1)} %param.199, bf16[512,1024]{1,0:T(8,128)(2,1)S(1)} %copy-done, bf16[512,4096]{1,0:T(8,128)(2,1)} %param.198), kind=kOutput, calls=%fused_computation | convolution fusion | flops 4303355904 | bytes 30408704 | tf_op jit(solution)/shard_map/dot_general | solution.py:31
  17.2 5.7 copy-done.2
  22.9 15.3 %convolution_bitcast_fusion = f32[32,1024]{1,0:T(8,128)S(1)} fusion(f32[1024,4096]{1,0:T(8,128)S(1)} %convert_add_fusion, f32[32,4096]{1,0:T(8,128)S(1)} %copy-done.7), kind=kOutput, calls=%fused_computation.3 | convolution fusion | flops 1610612736 | bytes 17432576 | tf_op jit(solution)/shard_map/dot_general | solution.py:39
  38.8 1.0 collective-permute-done
  39.8 3.1 collective-permute-start.1
  42.8 3.8 collective-permute-done.1
  46.7 1.8 collective-permute-start.2
  48.5 3.2 collective-permute-done.2
  51.7 1.9 collective-permute-start.3
  53.6 3.1 collective-permute-done.3
  56.8 3.3 collective-permute-start.4
  60.1 4.4 collective-permute-done.4
  86.2 0.9 convolution_bitcast_fusion.87
  88.8 0.9 convolution_bitcast_fusion.86
  91.4 0.9 convolution_bitcast_fusion.85
  94.0 0.9 convolution_bitcast_fusion.84
  112.1 0.9 convolution_bitcast_fusion.77
  145.8 14.1 %fusion.267 = f32[32,4096]{1,0:T(8,128)} fusion(f32[32,1024]{1,0:T(8,128)S(1)} %scatter.371, f32[1024,4096]{1,0:T(8,128)} %copy-done.2), kind=kOutput, calls=%fused_computation.560 | convolution fusion | flops 1610612736 | bytes 17432576 | tf_op jit(solution)/shard_map/dot_general | solution.py:51
  160.0 130.3 %all-reduce.7.cloned.1.call-done = f32[32,4096]{1,0:T(8,128)} async-done(((f32[32,4096]{1,0:T(8,128)}), f32[32,4096]{1,0:T(8,128)}) %all-reduce.7.cloned.1.call-update) | async-done | bytes 524304 | tf_op jit(solution)/shard_map/psum | solution.py:55
  290.3 18.7 %fusion.3 = f32[32,1024]{1,0:T(8,128)S(1)} fusion(f32[1024,4096]{1,0:T(8,128)} %copy-done.2, f32[32,4096]{1,0:T(8,128)} %all-reduce.7.cloned.1.call-done), kind=kOutput, calls=%fused_computation.103 | convolution fusion | flops 1610743808 | bytes 17432576 | tf_op jit(solution)/shard_map/dot_general | solution.py:39
  309.0 1.3 collective-permute-done.5
  310.4 1.5 collective-permute-start.6
  311.9 4.1 collective-permute-done.6
  316.0 1.5 collective-permute-start.7
  317.6 3.5 collective-permute-done.7
  321.1 1.5 collective-permute-start.8
  322.6 3.5 collective-permute-done.8
  326.1 1.5 collective-permute-start.9
  327.6 5.8 collective-permute-done.9
  376.3 0.9 convolution_bitcast_fusion.47
  415.2 13.9 %fusion.298 = f32[32,4096]{1,0:T(8,128)} fusion(f32[32,1024]{1,0:T(8,128)S(1)} %scatter.425, f32[1024,4096]{1,0:T(8,128)} %copy-done.2), kind=kOutput, calls=%fused_computation.591 | convolution fusion | flops 1610612736 | bytes 17432576 | tf_op jit(solution)/shard_map/dot_general | solution.py:51
  429.3 128.1 %all-reduce.9.cloned.1.call-done = f32[32,4096]{1,0:T(8,128)} async-done(((f32[32,4096]{1,0:T(8,128)}), f32[32,4096]{1,0:T(8,128)}) %all-reduce.9.cloned.1.call-update) | async-done | bytes 524304 | tf_op jit(solution)/shard_map/psum | solution.py:55
  557.4 18.7 %fusion.1 = f32[32,1024]{1,0:T(8,128)S(1)} fusion(f32[1024,4096]{1,0:T(8,128)} %copy-done.2, f32[32,4096]{1,0:T(8,128)} %all-reduce.9.cloned.1.call-done), kind=kOutput, calls=%fused_computation.101 | convolution fusion | flops 1610743808 | bytes 17432576 | tf_op jit(solution)/shard_map/dot_general | solution.py:39
  576.1 1.3 collective-permute-done.10
  577.5 1.5 collective-permute-start.11
  579.0 4.1 collective-permute-done.11
  583.1 1.5 collective-permute-start.12
  584.7 3.5 collective-permute-done.12
  588.2 1.5 collective-permute-start.13
  589.7 3.5 collective-permute-done.13
  593.2 1.5 collective-permute-start.14
  594.8 5.8 collective-permute-done.14
  682.1 13.9 %fusion.329 = f32[32,4096]{1,0:T(8,128)} fusion(f32[32,1024]{1,0:T(8,128)S(1)} %scatter.479, f32[1024,4096]{1,0:T(8,128)} %copy-done.2), kind=kOutput, calls=%fused_computation.622 | convolution fusion | flops 1610612736 | bytes 17432576 | tf_op jit(solution)/shard_map/dot_general | solution.py:51
  696.0 128.2 %all-reduce.11.cloned.1.call-done = f32[32,4096]{1,0:T(8,128)} async-done(((f32[32,4096]{1,0:T(8,128)}), f32[32,4096]{1,0:T(8,128)}) %all-reduce.11.cloned.1.call-update) | async-done | bytes 524304 | tf_op jit(solution)/shard_map/psum | solution.py:57
  824.3 1.1 broadcast_multiply_fusion
  825.4 13.6 %fusion.330 = f32[1024,4096]{1,0:T(8,128)S(1)} fusion(f32[32,1024]{1,0:T(8,128)S(1)} %scatter.479, f32[32,4096]{1,0:T(8,128)S(1)} %broadcast_multiply_fusion), kind=kOutput, calls=%fused_computation.623 | convolution fusion | flops 1610612736 | bytes 17432576 | tf_op jit(solution)/shard_map/dot_general | solution.py:20
  839.0 9.6 %fusion = bf16[1,1024,4096]{2,1,0:T(8,128)(2,1)} fusion(f32[1024,4096]{1,0:T(8,128)} %copy-done.2, f32[1024,4096]{1,0:T(8,128)S(1)} %fusion.330), kind=kLoop, calls=%fused_computation.2 | loop fusion | flops 8388608 | bytes 41943040 | tf_op jit(solution)/shard_map/broadcast_in_dim | solution.py:61
  (521 shorter events, 172.2 us)
Async XLA Ops:
  7.2 1.2 copy-start
  7.2 15.7 %copy-start.7 = (f32[32,4096]{1,0:T(8,128)S(1)}, f32[32,4096]{1,0:T(8,128)}, u32[]{:S(2)}) copy-start(f32[32,4096]{1,0:T(8,128)} %param.200) | copy-start | bytes 1572868
  7.2 283.1 %all-reduce.7.cloned.1.call-start = ((), (), s32[]{:S(2)}) async-start(), calls=%async_computation | async-start | bytes 1048576 | tf_op jit(solution)/shard_map/psum | solution.py:55
  17.2 5.7 copy-start.2
  38.2 1.5 collective-permute-start
  39.8 6.9 collective-permute-start.1
  46.7 5.0 collective-permute-start.2
  51.7 5.0 collective-permute-start.3
  56.8 7.7 collective-permute-start.4
  64.5 3.6 copy-start.4
  159.9 397.4 %all-reduce.9.cloned.1.call-start = ((), (), s32[]{:S(2)}) async-start(), calls=%async_computation.1 | async-start | bytes 1048576 | tf_op jit(solution)/shard_map/psum | solution.py:55
  308.9 1.4 collective-permute-start.5
  310.4 5.6 collective-permute-start.6
  316.0 5.0 collective-permute-start.7
  321.1 5.0 collective-permute-start.8
  326.1 7.3 collective-permute-start.9
  333.5 3.6 copy-start.5
  429.1 395.2 %all-reduce.11.cloned.1.call-start = ((), (), s32[]{:S(2)}) async-start(), calls=%async_computation.2 | async-start | bytes 1048576 | tf_op jit(solution)/shard_map/psum | solution.py:57
  576.1 1.4 collective-permute-start.10
  577.5 5.6 collective-permute-start.11
  583.1 5.0 collective-permute-start.12
  588.2 5.0 collective-permute-start.13
  593.2 7.3 collective-permute-start.14
  600.6 3.6 copy-start.3
  825.3 23.2 %copy-start.6 = (f32[32,4096]{1,0:T(8,128)}, f32[32,4096]{1,0:T(8,128)S(1)}, u32[]{:S(2)}) copy-start(f32[32,4096]{1,0:T(8,128)S(1)} %broadcast_multiply_fusion) | copy-start | bytes 1572868
  825.4 24.1 %copy-start.1 = (bf16[512,1024]{1,0:T(8,128)(2,1)S(1)}, bf16[512,1024]{1,0:T(8,128)(2,1)}, u32[]{:S(2)}) copy-start(bf16[512,1024]{1,0:T(8,128)(2,1)} %param.197) | copy-start | bytes 3145732
  839.0 9.6 %copy-start.8 = (f32[1024,128]{1,0:T(8,128)S(1)}, f32[1024,128]{1,0:T(8,128)}, u32[]{:S(2)}) copy-start(f32[1024,128]{1,0:T(8,128)} %param.201) | copy-start | bytes 1572868
Sparse Core Ops, SparseCore 0:
  160.0 130.1 all-reduce.6
  429.2 128.1 all-reduce.8
  696.1 128.0 all-reduce.10
